TPU v7x, 32 devices: a whole 2x2x4 slice. The times are simulated.
32 devices in a mesh: mb: 4 (over z), tp: 2 (over y), dp: 4 (over x, core).
Axes of the slice: x: 2, y: 2, z: 4, core: 2. Of those that a mesh axis runs over, the one named last changes fastest.
Arguments:
- hidden: bfloat16 [4, 8, 512, 7168], P('dp', 'mb', None, 'tp'), may hold values from -6 to 6
- latent: bfloat16 [4, 8, 512, 512], P('dp', 'mb', None, 'tp'), may hold values from -6 to 6
- out_grad: bfloat16 [4, 8, 512, 16384], P('dp', 'mb', None, 'tp'), may hold values from -0.059814453 to 0.059814453
- up_weight: bfloat16 [512, 16384], P(None, 'tp'), may hold values from -0.046875 to 0.046875
- mb_tokens: int32 [4, 8], P('dp'), may hold values from 128 to 512, as said below
- slot_mb: int32 [4, 8], P('dp', 'mb'), may hold values from 0 to 7, each once within a row
Outputs:
- up_grad: float32 [512, 16384], P(('mb', 'dp'), 'tp')
- running_down: float32 [4, 7168, 512], P('mb', 'tp', 'dp')
Inputs may be any that keep to these rules, and one draw needn't show every extreme that they name: `mb_tokens`: each count is a multiple of 128; in every group some microbatch has exactly 512 tokens. `slot_mb`: each row is a permutation of the microbatch numbers.
All inputs are finite; a program needn't handle non-finite values.
Results may differ from a plain program's by a relative error of at most 0.005.
Values may be sent and summed in bfloat16 or wider, within the bound.
A program may use at most 128 MiB of HBM per device.

v0:
```python
import jax
import jax.numpy as jnp
from jax import lax
from jax.sharding import PartitionSpec as P


def carried_in(part, axis, combine, identity):
    place = lax.axis_index(axis)
    gathered = lax.all_gather(part, axis)
    state = jnp.zeros_like(part) + jnp.asarray(identity, part.dtype)

    def one(lap, state):
        return combine(state, lax.dynamic_index_in_dim(gathered, lap, 0, False))

    return lax.fori_loop(0, place, one, state)


def add_terms(earlier, later):
    return earlier + later


def local(hidden, latent, out_grad, up_weight, mb_tokens, slot_mb):
    slot_count = hidden.shape[1]
    capacity = hidden.shape[2]
    micro_count = mb_tokens.shape[1]
    row_total = slot_count * capacity
    slot_ids = slot_mb[0]
    lookup = slot_ids[:, None] == jnp.arange(micro_count, dtype=jnp.int32)[None, :]
    counts = jnp.sum(jnp.where(lookup, mb_tokens[0][None, :], 0), axis=1)
    valid_rows = jnp.arange(capacity, dtype=jnp.int32)[None, :] < counts[:, None]
    masked_grads = jnp.where(valid_rows[:, :, None], out_grad[0], jnp.zeros((), out_grad.dtype))
    masked_grads = masked_grads.reshape(row_total, -1)
    factors = lax.all_gather(latent[0].reshape(row_total, -1), "tp", axis=1, tiled=True)
    partial_latent = lax.dot_general(
        masked_grads, up_weight, (((1,), (1,)), ((), ())), preferred_element_type=jnp.float32
    )
    latent_grad = lax.psum(partial_latent, "tp").astype(jnp.bfloat16)
    up_grad = lax.psum_scatter(
        lax.dot_general(
            factors, masked_grads, (((0,), (0,)), ((), ())), preferred_element_type=jnp.float32
        ),
        ("mb", "dp"),
        scatter_dimension=0,
        tiled=True,
    )
    hidden_rows = hidden[0].reshape(row_total, -1)
    down_term = lax.dot_general(
        hidden_rows, latent_grad, (((0,), (0,)), ((), ())), preferred_element_type=jnp.float32
    )
    down_share = lax.psum_scatter(down_term, "dp", scatter_dimension=1, tiled=True)
    earlier = carried_in(down_share, "mb", add_terms, jnp.zeros_like(down_share))
    running = earlier + down_share
    return (up_grad, running[None])


def solution(mesh):
    return jax.shard_map(
        local,
        mesh=mesh,
        in_specs=(
            P("dp", "mb", None, "tp"),
            P("dp", "mb", None, "tp"),
            P("dp", "mb", None, "tp"),
            P(None, "tp"),
            P("dp", None),
            P("dp", "mb"),
        ),
        out_specs=(P(("mb", "dp"), "tp"), P("mb", "tp", "dp")),
        check_vma=False,
    )
```

profile of v0, /device:TPU:0, one launch (start us, length us, event | category | flops | bytes accessed | tf_op | source)
XLA Modules:
  0.0 487.2 jit_solution(6459500900742012512)
XLA Ops:
  8.0 0.0 reduce-scatter.5.cloned.1.call-start
  8.0 0.9 fusion.1
  8.9 0.1 iota_compare_fusion
  9.0 14.0 %bitcast_select_fusion = bf16[1024,8192]{1,0:T(8,128)(2,1)} fusion(bf16[1,2,512,8192]{3,2,1,0:T(8,128)(2,1)} %param.10, pred[1024]{0:T(1024)(128)(4,1)S(1)} %lt.30), kind=kLoop, calls=%fused_computation.1 | loop fusion | flops 8388608 | bytes 33555456 | tf_op jit(solution)/shard_map/jit(_where)/select_n | solution.py:31
  23.0 14.4 %fusion.2 = f32[1024,512]{1,0:T(8,128)S(1)} fusion(bf16[1024,8192]{1,0:T(8,128)(2,1)} %bitcast_select_fusion, bf16[512,8192]{1,0:T(8,128)(2,1)} %param.11), kind=kOutput, calls=%fused_computation.9 | convolution fusion | flops 8589934592 | bytes 27262976 | tf_op jit(solution)/shard_map/dot_general | solution.py:34
  37.4 54.2 %all-reduce.1 = bf16[1024,512]{1,0:T(8,128)(2,1)S(1)} all-reduce(f32[1024,512]{1,0:T(8,128)S(1)} %fusion.2), channel_id=1, replica_groups=mesh['mb'=4,'tp'=2,'dp'=4] {'tp'}, use_global_device_ids=true, to_apply=%region_2.3 | all-reduce | flops 524288 | bytes 3145728 | tf_op jit(solution)/shard_map/psum | solution.py:37
  91.7 9.2 %convolution_bitcast_fusion.1 = f32[3584,512]{0,1:T(8,128)} fusion(bf16[1024,3584]{1,0:T(8,128)(2,1)} %bitcast.25, bf16[1024,512]{1,0:T(8,128)(2,1)S(1)} %all-reduce.1), kind=kOutput, calls=%fused_computation.3 | convolution fusion | flops 3758096384 | bytes 15728640 | tf_op jit(solution)/shard_map/dot_general | solution.py:47
  100.8 0.0 reduce-scatter.5.cloned.1.call-update
  100.8 0.0 all-gather.4.cloned.1.call-start
  100.9 0.5 all-gather.4.cloned.1.call-update
  101.4 0.0 all-gather.6.cloned.1.call-start
  101.5 65.8 %reduce-scatter.5.cloned.1.call-done = f32[3584,128]{0,1:T(8,128)} async-done(((f32[3584,512]{0,1:T(8,128)}), f32[3584,128]{0,1:T(8,128)}) %reduce-scatter.5.cloned.1.call-update) | async-done | bytes 1835024 | tf_op jit(solution)/shard_map/reduce_scatter | solution.py:50
  167.2 0.0 all-gather.6.cloned.1.call-update
  167.2 0.0 reduce-scatter.7.cloned.1.call-start
  167.3 0.0 all-gather.4.cloned.1.call-done
  167.3 16.0 %convolution_bitcast_fusion = f32[512,8192]{0,1:T(8,128)} fusion(bf16[1024,8192]{1,0:T(8,128)(2,1)} %bitcast_select_fusion, bf16[1024,512]{1,0:T(8,128)(2,1)} %all-gather.4.cloned.1.call-done), kind=kOutput, calls=%fused_computation.2 | convolution fusion | flops 8589934592 | bytes 34603008 | tf_op jit(solution)/shard_map/dot_general | solution.py:39
  183.3 17.5 %copy.21 = f32[512,8192]{1,0:T(8,128)} copy(f32[512,8192]{0,1:T(8,128)} %convolution_bitcast_fusion) | data formatting | bytes 33554432
  200.8 0.0 reduce-scatter.7.cloned.1.call-update
  200.8 98.9 %all-gather.6.cloned.1.call-done = f32[14336,128]{0,1:T(8,128)} async-done(((f32[3584,128]{0,1:T(8,128)}), f32[14336,128]{0,1:T(8,128)}) %all-gather.6.cloned.1.call-update) | async-done | bytes 7340048 | tf_op jit(solution)/shard_map/all_gather | solution.py:9
  299.7 8.6 %copy.20 = f32[14336,128]{1,0:T(8,128)} copy(f32[14336,128]{0,1:T(8,128)} %all-gather.6.cloned.1.call-done) | data formatting | bytes 14680064 | tf_op jit(solution)/shard_map/while | solution.py:15
  308.3 0.1 broadcast_in_dim.41
  308.5 1.7 copy.17
  310.2 3.0 add_bitcast_fusion
  313.2 1.7 copy.19
  314.9 164.7 %reduce-scatter.7.cloned.1.call-done = f32[32,8192]{1,0:T(8,128)} async-done(((f32[512,8192]{1,0:T(8,128)}), f32[32,8192]{1,0:T(8,128)}) %reduce-scatter.7.cloned.1.call-update) | async-done | bytes 1048592
  (2 shorter events, 0.0 us)
Async XLA Ops:
  8.0 159.2 %reduce-scatter.5.cloned.1.call-start = ((), (), s32[]{:S(2)}) async-start(), calls=%async_computation.3 | async-start | bytes 9175040 | tf_op jit(solution)/shard_map/reduce_scatter | solution.py:50
  100.8 66.5 %all-gather.4.cloned.1.call-start = ((), (), s32[]{:S(2)}) async-start(), calls=%async_computation.2 | async-start | bytes 1572864 | tf_op jit(solution)/shard_map/all_gather | solution.py:33
  101.4 198.3 %all-gather.6.cloned.1.call-start = ((), (), s32[]{:S(2)}) async-start(), calls=%async_computation.4 | async-start | bytes 9175040 | tf_op jit(solution)/shard_map/all_gather | solution.py:9
  167.2 312.4 %reduce-scatter.7.cloned.1.call-start = ((), (), s32[]{:S(2)}) async-start(), calls=%async_computation.5 | async-start | bytes 17825792
Sparse Core Ops, SparseCore 0:
  101.0 66.2 reduce-scatter.4
Sparse Core Ops, SparseCore 1:
  102.8 21.4 all-gather.3
  167.3 132.3 all-gather.5
  304.2 175.3 reduce-scatter.6
where the time goes:
time: 488 us; the launch traced here: 487 us
  waiting for transfers between devices  330 us (68%)
  blocking collectives  54.2 us (11%)
  matrix products  39.6 us (8%)
  local copies, waits for them, and re-layouts  29.6 us (6%)
  other arithmetic  18 us (4%)
  between operations  15.7 us (3%)
    unnamed x5, waiting for transfers between devices  165 us
    all_gather x1, waiting for transfers between devices, carried_in(): gathered = lax.all_gather(part, axis)  98.9 us
    reduce_scatter x1, waiting for transfers between devices, local(): lax.psum_scatter(down_term, 'dp', scatter_dimension=1, tiled=True)  65.8 us
    psum x1, blocking collectives, local(): latent_grad = lax.psum(partial_latent, 'tp').astype(jnp.bfloat16)  54.2 us
    unnamed x2, local copies, waits for them, and re-layouts  19.2 us
    dot_general x1, matrix products, local(): lax.dot_general(factors, masked_grads, (((0,), (0,)), ((), ())), preferre...  16 us
    dot_general x1, matrix products, local(): lax.dot_general(masked_grads, up_weight, (((1,), (1,)), ((), ())), prefer...  14.4 us
    select_n x1, other arithmetic, local(): jnp.where(valid_rows[:, :, None], out_grad[0], jnp.zeros((), out_grad.dty...  14 us
  transfers between devices with their start and end apart: 4, of which 3 were waited for; matrix products, arithmetic and copies ran while one was open for 10% of the time, Pallas kernels for 0%

commit v1 on v0

--- a/solution.py
+++ b/solution.py
@@ -34,7 +34,7 @@
     partial_latent = lax.dot_general(
         masked_grads, up_weight, (((1,), (1,)), ((), ())), preferred_element_type=jnp.float32
     )
-    latent_grad = lax.psum(partial_latent, "tp").astype(jnp.bfloat16)
+    latent_grad = lax.all_gather(partial_latent, axis_name="tp").sum(axis=0).astype(jnp.bfloat16)
     up_grad = lax.psum_scatter(
         lax.dot_general(
             factors, masked_grads, (((0,), (0,)), ((), ())), preferred_element_type=jnp.float32

time: 488 us -> 520 us (1.066)
  waiting for transfers between devices: 330 us -> 414 us
  blocking collectives: 54.2 us -> 0 us
    all_gather x0 -> x1, waiting for transfers between devices: none -> 59.6 us  [local(): lax.all_gather(partial_latent, axis_name='tp').sum(axis=0)]
    psum x1 -> x0, blocking collectives: 54.2 us -> none  [local(): latent_grad = lax.psum(partial_latent, 'tp').astype(jnp.bfloat16)]
    all_gather x1, waiting for transfers between devices: 0.02 us -> 22.6 us  [local(): lax.all_gather(latent[0].reshape(row_total, -1), 'tp', axis=1, tiled=True)]
    unnamed x5 -> x6, waiting for transfers between devices: 165 us -> 166 us
  transfers between devices with their start and end apart: 4 -> 5, of which waited for: 3 -> 5; matrix products, arithmetic and copies ran while one was open for 10% -> 9% of each run, Pallas kernels for 0% -> 0%
where the time goes in v1:
time: 520 us; the launch traced here: 519 us
  waiting for transfers between devices  414 us (80%)
  matrix products  41 us (8%)
  local copies, waits for them, and re-layouts  29.6 us (6%)
  other arithmetic  20.7 us (4%)
  between operations  13.8 us (3%)
    unnamed x6, waiting for transfers between devices  166 us
    all_gather x1, waiting for transfers between devices, carried_in(): gathered = lax.all_gather(part, axis)  100 us
    reduce_scatter x1, waiting for transfers between devices, local(): lax.psum_scatter(down_term, 'dp', scatter_dimension=1, tiled=True)  65.3 us
    all_gather x1, waiting for transfers between devices, local(): lax.all_gather(partial_latent, axis_name='tp').sum(axis=0)  59.6 us
    all_gather x1, waiting for transfers between devices, local(): lax.all_gather(latent[0].reshape(row_total, -1), 'tp', axis=1, tiled=True)  22.6 us
    unnamed x2, local copies, waits for them, and re-layouts  19.1 us
    dot_general x1, matrix products, local(): lax.dot_general(factors, masked_grads, (((0,), (0,)), ((), ())), preferre...  16 us
    dot_general x1, matrix products, local(): lax.dot_general(masked_grads, up_weight, (((1,), (1,)), ((), ())), prefer...  15.8 us
  transfers between devices with their start and end apart: 5, of which 5 were waited for; matrix products, arithmetic and copies ran while one was open for 9% of the time, Pallas kernels for 0%

profile of v1, /device:TPU:0, one launch (start us, length us, event | category | flops | bytes accessed | tf_op | source)
XLA Modules:
  0.0 519.0 jit_solution(15517648824346551574)
XLA Ops:
  7.2 0.0 all-gather.8.cloned.1.call-start
  7.2 0.9 fusion.1
  8.1 0.1 iota_compare_fusion
  8.2 14.0 %bitcast_select_fusion = bf16[1024,8192]{1,0:T(8,128)(2,1)} fusion(bf16[1,2,512,8192]{3,2,1,0:T(8,128)(2,1)} %param.10, pred[1024]{0:T(1024)(128)(4,1)S(1)} %lt.30), kind=kLoop, calls=%fused_computation.1 | loop fusion | flops 8388608 | bytes 33555456 | tf_op jit(solution)/shard_map/jit(_where)/select_n | solution.py:31
  22.1 15.8 %fusion.2 = f32[1024,512]{1,0:T(8,128)} fusion(bf16[1024,8192]{1,0:T(8,128)(2,1)} %bitcast_select_fusion, bf16[512,8192]{1,0:T(8,128)(2,1)} %param.11), kind=kOutput, calls=%fused_computation.9 | convolution fusion | flops 8589934592 | bytes 27262976 | tf_op jit(solution)/shard_map/dot_general | solution.py:34
  38.0 0.0 all-gather.8.cloned.1.call-update
  38.0 0.0 reduce-scatter.5.cloned.1.call-start
  38.0 59.6 %all-gather.8.cloned.1.call-done = f32[2048,512]{1,0:T(8,128)} async-done(((f32[1024,512]{1,0:T(8,128)}), f32[2048,512]{1,0:T(8,128)}) %all-gather.8.cloned.1.call-update) | async-done | bytes 4194320 | tf_op jit(solution)/shard_map/all_gather | solution.py:37
  97.6 2.8 reduce_sum.19
  100.4 9.2 %convolution_bitcast_fusion.1 = f32[3584,512]{0,1:T(8,128)} fusion(bf16[1024,3584]{1,0:T(8,128)(2,1)} %bitcast.26, bf16[1024,512]{1,0:T(8,128)(2,1)S(1)} %reduce_sum.19), kind=kOutput, calls=%fused_computation.3 | convolution fusion | flops 3758096384 | bytes 15728640 | tf_op jit(solution)/shard_map/dot_general | solution.py:47
  109.5 0.0 reduce-scatter.5.cloned.1.call-update
  109.5 0.0 all-gather.6.cloned.1.call-start
  109.6 0.7 all-gather.6.cloned.1.call-update
  110.3 0.0 all-gather.10.cloned.1.call-start
  110.3 65.3 %reduce-scatter.5.cloned.1.call-done = f32[3584,128]{0,1:T(8,128)} async-done(((f32[3584,512]{0,1:T(8,128)}), f32[3584,128]{0,1:T(8,128)}) %reduce-scatter.5.cloned.1.call-update) | async-done | bytes 1835024 | tf_op jit(solution)/shard_map/reduce_scatter | solution.py:50
  175.7 0.0 all-gather.10.cloned.1.call-update
  175.7 0.2 reduce-scatter.7.cloned.1.call-start
  175.9 22.6 %all-gather.6.cloned.1.call-done = bf16[1024,512]{1,0:T(8,128)(2,1)} async-done(((bf16[1024,256]{1,0:T(8,128)(2,1)}), bf16[1024,512]{1,0:T(8,128)(2,1)}) %all-gather.6.cloned.1.call-update) | async-done | bytes 1048592 | tf_op jit(solution)/shard_map/all_gather | solution.py:33
  198.5 16.0 %convolution_bitcast_fusion = f32[512,8192]{0,1:T(8,128)} fusion(bf16[1024,8192]{1,0:T(8,128)(2,1)} %bitcast_select_fusion, bf16[1024,512]{1,0:T(8,128)(2,1)} %all-gather.6.cloned.1.call-done), kind=kOutput, calls=%fused_computation.2 | convolution fusion | flops 8589934592 | bytes 34603008 | tf_op jit(solution)/shard_map/dot_general | solution.py:39
  214.5 17.5 %copy.21 = f32[512,8192]{1,0:T(8,128)} copy(f32[512,8192]{0,1:T(8,128)} %convolution_bitcast_fusion) | data formatting | bytes 33554432
  231.9 0.0 reduce-scatter.7.cloned.1.call-update
  231.9 100.5 %all-gather.10.cloned.1.call-done = f32[14336,128]{0,1:T(8,128)} async-done(((f32[3584,128]{0,1:T(8,128)}), f32[14336,128]{0,1:T(8,128)}) %all-gather.10.cloned.1.call-update) | async-done | bytes 7340048 | tf_op jit(solution)/shard_map/all_gather | solution.py:9
  332.4 8.7 %copy.20 = f32[14336,128]{1,0:T(8,128)} copy(f32[14336,128]{0,1:T(8,128)} %all-gather.10.cloned.1.call-done) | data formatting | bytes 14680064 | tf_op jit(solution)/shard_map/while | solution.py:15
  341.1 0.1 broadcast_in_dim.41
  341.2 1.7 copy.17
  342.9 3.0 add_bitcast_fusion
  345.9 1.7 copy.19
  347.6 164.9 %reduce-scatter.7.cloned.1.call-done = f32[32,8192]{1,0:T(8,128)} async-done(((f32[512,8192]{1,0:T(8,128)}), f32[32,8192]{1,0:T(8,128)}) %reduce-scatter.7.cloned.1.call-update) | async-done | bytes 1048592
  (2 shorter events, 0.0 us)
Async XLA Ops:
  7.2 90.4 %all-gather.8.cloned.1.call-start = ((), (), s32[]{:S(2)}) async-start(), calls=%async_computation.4 | async-start | bytes 6291456 | tf_op jit(solution)/shard_map/all_gather | solution.py:37
  38.0 137.7 %reduce-scatter.5.cloned.1.call-start = ((), (), s32[]{:S(2)}) async-start(), calls=%async_computation.3 | async-start | bytes 9175040 | tf_op jit(solution)/shard_map/reduce_scatter | solution.py:50
  109.5 88.9 %all-gather.6.cloned.1.call-start = ((), (), s32[]{:S(2)}) async-start(), calls=%async_computation.2 | async-start | bytes 1572864 | tf_op jit(solution)/shard_map/all_gather | solution.py:33
  110.3 222.1 %all-gather.10.cloned.1.call-start = ((), (), s32[]{:S(2)}) async-start(), calls=%async_computation.5 | async-start | bytes 9175040 | tf_op jit(solution)/shard_map/all_gather | solution.py:9
  175.7 336.8 %reduce-scatter.7.cloned.1.call-start = ((), (), s32[]{:S(2)}) async-start(), calls=%async_computation.6 | async-start | bytes 17825792
Sparse Core Ops, SparseCore 0:
  38.1 59.4 all-gather.7
  109.7 65.9 reduce-scatter.4
  177.2 21.2 all-gather.5
  199.9 132.4 all-gather.9
  336.9 175.5 reduce-scatter.6
